TPU v7x, 32 devices: a whole 2x2x4 slice. The times are simulated.
32 devices in a mesh: member: 16 (over z, y, core), slab: 2 (over x).
Axes of the slice: x: 2, y: 2, z: 4, core: 2. Of those that a mesh axis runs over, the one named last changes fastest.
Arguments:
- checkpoint: float32 [16, 2, 4, 256, 256], P('member', None, 'slab'), may hold values from 0 to 1
- adjoint_late: float32 [16, 2, 4, 256, 256], P('member', None, 'slab'), may hold values from -6 to 6
- rate_params: float32 [64, 64], replicated, may hold values from 0.02 to 0.1
- perturbation: float32 [16, 64, 64], P('member'), may hold values from -0.5 to 0.5
Outputs:
- adjoint_early: float32 [16, 2, 4, 256, 256], P('member', None, 'slab')
- param_grad: float32 [64, 64], replicated
All inputs are finite; a program needn't handle non-finite values.
Results may differ from a plain program's by a relative error of at most 0.00002.
Values sent between devices are 32-bit elements; how exact they have to be, the bound alone decides.
A program may use at most 64 MiB of HBM per device.

v0:
```python
import jax
import jax.numpy as jnp
from jax import lax
from jax.sharding import PartitionSpec as P

PX = 64
PY = 64
SX = 4
SY = 4
NX = 256
NY = 256


feed_rate = 0.035
substrate_diffusion = 0.16
activator_diffusion = 0.08


def with_halo(cells, sides, width):
    for axis, dim in sides:
        count = lax.axis_size(axis)
        ends = count - 1
        head = lax.slice_in_dim(cells, 0, width, axis=dim)
        tail = lax.slice_in_dim(cells, cells.shape[dim] - width, cells.shape[dim], axis=dim)
        cells = jnp.concatenate(
            [
                lax.ppermute(tail, axis, [(i, (i + 1) % count) for i in range(ends)]),
                cells,
                lax.ppermute(head, axis, [((i + 1) % count, i) for i in range(ends)]),
            ],
            axis=dim,
        )
    return cells


def laplace_rim(extended):
    padded = jnp.pad(extended, ((0, 0), (0, 0), (1, 1), (1, 1)))
    center = padded[:, 1:-1, 1:-1, 1:-1]
    summed = padded[:, 2:, 1:-1, 1:-1] + padded[:, :-2, 1:-1, 1:-1]
    summed = summed + padded[:, 1:-1, 2:, 1:-1] + padded[:, 1:-1, :-2, 1:-1]
    summed = summed + padded[:, 1:-1, 1:-1, 2:] + padded[:, 1:-1, 1:-1, :-2]
    return summed - 6.0 * center


def advance(extended, decay_rate):
    laplace = laplace_rim(extended)
    u_field = extended[0, 1:-1]
    v_field = extended[1, 1:-1]
    reaction = u_field * v_field * v_field
    u_new = u_field + substrate_diffusion * laplace[0] - reaction + feed_rate * (1.0 - u_field)
    v_new = (
        v_field + activator_diffusion * laplace[1] + reaction - (feed_rate + decay_rate) * v_field
    )
    return jnp.stack([u_new, v_new])


def pull_back(status, adjoint_ext, decay_rate):
    laplace = laplace_rim(adjoint_ext)
    adj_u = adjoint_ext[0, 1:-1]
    adj_v = adjoint_ext[1, 1:-1]
    uv_prod = status[0] * status[1]
    v_square = status[1] * status[1]
    new_u = (
        adj_u + substrate_diffusion * laplace[0] - (v_square + feed_rate) * adj_u + v_square * adj_v
    )
    new_v = (
        adj_v
        + activator_diffusion * laplace[1]
        - 2.0 * uv_prod * adj_u
        + (2.0 * uv_prod - feed_rate - decay_rate) * adj_v
    )
    return jnp.stack([new_u, new_v])


def expand_params(table):
    return jnp.broadcast_to(table[:, None, :, None], (PX, SX, PY, SY)).reshape(NX, NY)


def patch_total(field):
    return jnp.sum(field.reshape(PX, SX, PY, SY), axis=(1, 3))


def local(checkpoint, adjoint_late, rate_params, perturbation):
    start_state = checkpoint[0]
    adjoint_two = adjoint_late[0]
    factor = 1.0 + perturbation[0]
    decay_rate = expand_params(rate_params * factor)
    member_count = lax.axis_size("member")
    state_ext, adjoint_ext_two = (
        with_halo(start_state, (("slab", 1),), 1),
        with_halo(adjoint_two, (("slab", 1),), 1),
    )
    middle = advance(state_ext, decay_rate)
    adjoint_one = pull_back(middle, adjoint_ext_two, decay_rate)
    first_term = -jnp.sum(middle[1] * adjoint_two[1], 0)
    adjoint_ext = with_halo(adjoint_one, (("slab", 1),), 1)
    adjoint_zero = pull_back(start_state, adjoint_ext, decay_rate)
    second = -jnp.sum(start_state[1] * adjoint_one[1], 0)
    param_grad = (
        lax.psum(patch_total(first_term + second) * factor, ("member", "slab")) / member_count
    )
    return (adjoint_zero[None], param_grad)


def solution(mesh):
    return jax.shard_map(
        local,
        mesh=mesh,
        in_specs=(
            P("member", None, "slab", None, None),
            P("member", None, "slab", None, None),
            P(),
            P("member", None, None),
        ),
        out_specs=(P("member", None, "slab", None, None), P()),
        check_vma=False,
    )
```

profile of v0, /device:TPU:0, one launch (start us, length us, event | category | flops | bytes accessed | tf_op | source)
XLA Modules:
  0.0 109.7 jit_solution(6081477376851431871)
XLA Ops:
  0.6 0.0 copy-start.5
  0.6 0.0 copy-start.4
  0.6 2.3 %fusion.44 = (f32[2,1,256,256]{3,2,1,0:T(8,128)}, f32[2,1,256,256]{3,2,1,0:T(8,128)}) fusion(f32[2,2,256,256]{3,2,1,0:T(8,128)} %bitcast.149), kind=kLoop, calls=%fused_computation.112 | loop fusion | bytes 2097152 | tf_op jit(solution)/shard_map/slice | solution.py:24
  2.9 1.3 %collective-permute-start = (f32[2,1,256,256]{3,2,1,0:T(8,128)}, f32[2,1,256,256]{3,2,1,0:T(8,128)S(1)}, u32[]{:S(2)}, u32[]{:S(2)}) collective-permute-start(f32[2,1,256,256]{3,2,1,0:T(8,128)} %get-tuple-element.13), channel_id=1, source_target_pairs={{1,0},{3,2},{5,4},{7,6},{9,8},{11,10},{13,12},{15,14},{17,16},{19,... | collective-permute-start | bytes 1572872 | tf_op jit(solution)/shard_map/ppermute | solution.py:29
  4.2 4.9 %collective-permute-start.1 = (f32[2,1,256,256]{3,2,1,0:T(8,128)}, f32[2,1,256,256]{3,2,1,0:T(8,128)S(1)}, u32[]{:S(2)}, u32[]{:S(2)}) collective-permute-start(f32[2,1,256,256]{3,2,1,0:T(8,128)} %get-tuple-element.12), channel_id=1, source_target_pairs={{0,1},{2,3},{4,5},{6,7},{8,9},{10,11},{12,13},{14,15},{16,17},{18,... | collective-permute-start | bytes 1572872 | tf_op jit(solution)/shard_map/ppermute | solution.py:27
  9.1 2.4 %fusion.43 = (f32[2,1,256,256]{3,2,1,0:T(8,128)}, f32[2,1,256,256]{3,2,1,0:T(8,128)}) fusion(f32[2,2,256,256]{3,2,1,0:T(8,128)} %bitcast.146), kind=kLoop, calls=%fused_computation.111 | loop fusion | bytes 2097152 | tf_op jit(solution)/shard_map/slice | solution.py:24
  11.5 1.3 %collective-permute-start.2 = (f32[2,1,256,256]{3,2,1,0:T(8,128)}, f32[2,1,256,256]{3,2,1,0:T(8,128)S(1)}, u32[]{:S(2)}, u32[]{:S(2)}) collective-permute-start(f32[2,1,256,256]{3,2,1,0:T(8,128)} %get-tuple-element.11), channel_id=1, source_target_pairs={{1,0},{3,2},{5,4},{7,6},{9,8},{11,10},{13,12},{15,14},{17,16},{19,... | collective-permute-start | bytes 1572872 | tf_op jit(solution)/shard_map/ppermute | solution.py:29
  12.8 5.4 %collective-permute-start.3 = (f32[2,1,256,256]{3,2,1,0:T(8,128)}, f32[2,1,256,256]{3,2,1,0:T(8,128)}, u32[]{:S(2)}, u32[]{:S(2)}) collective-permute-start(f32[2,1,256,256]{3,2,1,0:T(8,128)} %get-tuple-element.10), channel_id=1, source_target_pairs={{0,1},{2,3},{4,5},{6,7},{8,9},{10,11},{12,13},{14,15},{16,17},{18,... | collective-permute-start | bytes 1572872 | tf_op jit(solution)/shard_map/ppermute | solution.py:27
  18.2 0.0 copy-done.5
  18.2 0.0 copy-done.4
  18.2 3.8 %broadcast_in_dim.4 = f32[64,4,64,4]{3,2,1,0:T(8,128)} broadcast(f32[64,64]{1,0:T(8,128)S(1)} %bitcast_multiply_fusion.13), dimensions={0,2} | broadcast | bytes 278528 | tf_op jit(solution)/shard_map/broadcast_in_dim | solution.py:76
  22.0 0.0 copy-start.1
  22.0 8.4 %reshape.133 = f32[256,256]{1,0:T(8,128)S(1)} reshape(f32[64,4,64,4]{3,2,1,0:T(8,128)} %broadcast_in_dim.4) | data formatting | bytes 524288 | tf_op jit(solution)/shard_map/reshape | solution.py:76
  30.4 0.0 collective-permute-done
  30.4 0.0 copy-start.2
  30.4 0.0 collective-permute-done.1
  30.5 0.8 copy-done.2
  31.2 0.0 copy-start.3
  31.2 0.8 copy-done.3
  32.0 0.0 copy-done.1
  32.0 1.4 %select_maximum_fusion.5 = f32[2,4,258,258]{3,2,1,0:T(8,128)S(1)} fusion(f32[2,1,256,256]{3,2,1,0:T(8,128)S(1)} %collective-permute-done, f32[2,2,256,256]{3,2,1,0:T(8,128)S(1)} %bitcast.150, f32[2,1,256,256]{3,2,1,0:T(8,128)S(1)} %collective-permute-done.1), kind=kLoop, calls=%fused_computation.9 | loop fusion | flops 7987680 | bytes 4227200 | tf_op jit(solution)/shard_map/concatenate | solution.py:25
  33.5 0.0 copy-start
  33.5 2.2 %fusion.8 = f32[2,2,256,256]{3,2,1,0:T(8,128)S(1)} fusion(f32[2,4,258,258]{3,2,1,0:T(8,128)S(1)} %select_maximum_fusion.5, f32[2,2,256,256]{3,2,1,0:T(8,128)S(1)} %bitcast.151, f32[2,1,256,256]{3,2,1,0:T(8,128)} %copy-done.3, f32[2,1,256,256]{3,2,1,0:T(8,128)} %copy-done.2), kind=kLoop, calls=%fused_computation.39 | loop fusion | flops 2359296 | bytes 7340032 | tf_op jit(solution)/shard_map/sub | solution.py:42
  35.7 0.0 collective-permute-done.2
  35.7 0.0 collective-permute-done.3
  35.7 0.0 copy-done
  35.7 2.4 %select_maximum_fusion.3 = f32[2,4,258,258]{3,2,1,0:T(8,128)S(1)} fusion(f32[2,1,256,256]{3,2,1,0:T(8,128)S(1)} %collective-permute-done.2, f32[2,2,256,256]{3,2,1,0:T(8,128)S(1)} %bitcast.147, f32[2,1,256,256]{3,2,1,0:T(8,128)} %collective-permute-done.3), kind=kLoop, calls=%fused_computation.7 | loop fusion | flops 7987680 | bytes 4227200 | tf_op jit(solution)/shard_map/concatenate | solution.py:25
  38.2 2.0 %fusion.6 = f32[2,2,256,256]{3,2,1,0:T(8,128)S(1)} fusion(f32[2,4,258,258]{3,2,1,0:T(8,128)S(1)} %select_maximum_fusion.3, f32[2,2,256,256]{3,2,1,0:T(8,128)S(1)} %bitcast.148, f32[2,1,256,256]{3,2,1,0:T(8,128)} %collective-permute-done.3, f32[2,1,256,256]{3,2,1,0:T(8,128)S(1)} %collective-permute-done.2), kind=kLoop, calls=%fused_computation.31 | loop fusion | flops 2359296 | bytes 7340032 | tf_op jit(solution)/shard_map/sub | solution.py:42
  40.2 0.3 fusion.20
  40.4 0.5 fusion.29
  40.9 0.4 fusion.34
  41.3 1.1 fusion.11
  42.4 1.3 %collective-permute-start.4 = (f32[2,1,256,256]{3,2,1,0:T(8,128)}, f32[2,1,256,256]{3,2,1,0:T(8,128)S(1)}, u32[]{:S(2)}, u32[]{:S(2)}) collective-permute-start(f32[2,1,256,256]{3,2,1,0:T(8,128)} %get-tuple-element.9), channel_id=1, source_target_pairs={{1,0},{3,2},{5,4},{7,6},{9,8},{11,10},{13,12},{15,14},{17,16},{19,... | collective-permute-start | bytes 1572872 | tf_op jit(solution)/shard_map/ppermute | solution.py:29
  43.7 4.6 %collective-permute-start.5 = (f32[2,1,256,256]{3,2,1,0:T(8,128)}, f32[2,1,256,256]{3,2,1,0:T(8,128)S(1)}, u32[]{:S(2)}, u32[]{:S(2)}) collective-permute-start(f32[2,1,256,256]{3,2,1,0:T(8,128)} %get-tuple-element.8), channel_id=1, source_target_pairs={{0,1},{2,3},{4,5},{6,7},{8,9},{10,11},{12,13},{14,15},{16,17},{18,... | collective-permute-start | bytes 1572872 | tf_op jit(solution)/shard_map/ppermute | solution.py:27
  48.3 0.8 negate_add_fusion
  49.0 10.8 %add.226 = f32[64,4,64,4]{3,2,1,0:T(8,128)} reshape(f32[256,256]{1,0:T(8,128)} %negate_add_fusion) | data formatting | bytes 524288 | tf_op jit(solution)/shard_map/add | solution.py:100
  59.9 4.0 %reduce_sum.29 = f32[64,64]{1,0:T(8,128)S(1)} reduce(f32[64,4,64,4]{3,2,1,0:T(8,128)} %add.226, f32[]{:T(128)} %constant.9.clone.1), dimensions={1,3}, to_apply=%region_2.3 | reduce | flops 61440 | bytes 278532 | tf_op jit(solution)/shard_map/reduce_sum | solution.py:80
  63.9 41.0 %psum.7 = f32[64,64]{1,0:T(8,128)S(1)} all-reduce(f32[64,64]{1,0:T(8,128)S(1)} %bitcast_multiply_fusion.12), channel_id=1, replica_groups=mesh['member'=16,'slab'=2] {'member','slab'}, use_global_device_ids=true, to_apply=%region_3.4 | all-reduce | flops 4096 | bytes 32768 | tf_op jit(solution)/shard_map/psum | solution.py:100
  104.9 0.6 broadcast_multiply_fusion
  105.5 0.0 collective-permute-done.4
  105.5 0.0 collective-permute-done.5
  105.5 1.9 %select_maximum_fusion = f32[2,4,258,258]{3,2,1,0:T(8,128)S(1)} fusion(f32[2,1,256,256]{3,2,1,0:T(8,128)S(1)} %collective-permute-done.4, f32[2,1,256,256]{3,2,1,0:T(8,128)S(1)} %collective-permute-done.5, f32[1,2,256,256]{3,2,1,0:T(8,128)S(1)} %fusion.34, f32[1,2,256,256]{3,2,1,0:T(8,128)S(1)} %get-tuple-element.4), kind=kLoop, calls=%fused_computation.4 | loop fusion | flops 9585216 | bytes 4227200 | tf_op jit(solution)/shard_map/concatenate | solution.py:25
  107.4 0.9 fusion.4
  108.4 0.3 fusion.17
  108.7 1.0 maximum_bitcast_fusion
  (3 shorter events, 0.0 us)
Async XLA Ops:
  0.6 17.5 %copy-start.5 = (f32[64,64]{1,0:T(8,128)S(1)}, f32[64,64]{1,0:T(8,128)}, u32[]{:S(2)}) copy-start(f32[64,64]{1,0:T(8,128)} %param.6) | copy-start | bytes 49156
  0.6 17.5 %copy-start.4 = (f32[1,64,64]{2,1,0:T(8,128)S(1)}, f32[1,64,64]{2,1,0:T(8,128)}, u32[]{:S(2)}) copy-start(f32[1,64,64]{2,1,0:T(8,128)} %param.7) | copy-start | bytes 49156
  2.9 27.5 %collective-permute-start = (f32[2,1,256,256]{3,2,1,0:T(8,128)}, f32[2,1,256,256]{3,2,1,0:T(8,128)S(1)}, u32[]{:S(2)}, u32[]{:S(2)}) collective-permute-start(f32[2,1,256,256]{3,2,1,0:T(8,128)} %get-tuple-element.13), channel_id=1, source_target_pairs={{1,0},{3,2},{5,4},{7,6},{9,8},{11,10},{13,12},{15,14},{17,16},{19,... | collective-permute-start | bytes 1572872 | tf_op jit(solution)/shard_map/ppermute | solution.py:29
  4.2 26.3 %collective-permute-start.1 = (f32[2,1,256,256]{3,2,1,0:T(8,128)}, f32[2,1,256,256]{3,2,1,0:T(8,128)S(1)}, u32[]{:S(2)}, u32[]{:S(2)}) collective-permute-start(f32[2,1,256,256]{3,2,1,0:T(8,128)} %get-tuple-element.12), channel_id=1, source_target_pairs={{0,1},{2,3},{4,5},{6,7},{8,9},{10,11},{12,13},{14,15},{16,17},{18,... | collective-permute-start | bytes 1572872 | tf_op jit(solution)/shard_map/ppermute | solution.py:27
  11.5 24.2 %collective-permute-start.2 = (f32[2,1,256,256]{3,2,1,0:T(8,128)}, f32[2,1,256,256]{3,2,1,0:T(8,128)S(1)}, u32[]{:S(2)}, u32[]{:S(2)}) collective-permute-start(f32[2,1,256,256]{3,2,1,0:T(8,128)} %get-tuple-element.11), channel_id=1, source_target_pairs={{1,0},{3,2},{5,4},{7,6},{9,8},{11,10},{13,12},{15,14},{17,16},{19,... | collective-permute-start | bytes 1572872 | tf_op jit(solution)/shard_map/ppermute | solution.py:29
  12.8 23.0 %collective-permute-start.3 = (f32[2,1,256,256]{3,2,1,0:T(8,128)}, f32[2,1,256,256]{3,2,1,0:T(8,128)}, u32[]{:S(2)}, u32[]{:S(2)}) collective-permute-start(f32[2,1,256,256]{3,2,1,0:T(8,128)} %get-tuple-element.10), channel_id=1, source_target_pairs={{0,1},{2,3},{4,5},{6,7},{8,9},{10,11},{12,13},{14,15},{16,17},{18,... | collective-permute-start | bytes 1572872 | tf_op jit(solution)/shard_map/ppermute | solution.py:27
  22.0 10.0 %copy-start.1 = (f32[1,2,2,256,256]{4,3,2,1,0:T(8,128)S(1)}, f32[1,2,2,256,256]{4,3,2,1,0:T(8,128)}, u32[]{:S(2)}) copy-start(f32[1,2,2,256,256]{4,3,2,1,0:T(8,128)} %param.5) | copy-start | bytes 3145732
  30.4 0.8 copy-start.2
  31.2 0.8 copy-start.3
  33.5 2.3 %copy-start = (f32[1,2,2,256,256]{4,3,2,1,0:T(8,128)S(1)}, f32[1,2,2,256,256]{4,3,2,1,0:T(8,128)}, u32[]{:S(2)}) copy-start(f32[1,2,2,256,256]{4,3,2,1,0:T(8,128)} %param.4) | copy-start | bytes 3145732
  42.4 63.2 %collective-permute-start.4 = (f32[2,1,256,256]{3,2,1,0:T(8,128)}, f32[2,1,256,256]{3,2,1,0:T(8,128)S(1)}, u32[]{:S(2)}, u32[]{:S(2)}) collective-permute-start(f32[2,1,256,256]{3,2,1,0:T(8,128)} %get-tuple-element.9), channel_id=1, source_target_pairs={{1,0},{3,2},{5,4},{7,6},{9,8},{11,10},{13,12},{15,14},{17,16},{19,... | collective-permute-start | bytes 1572872 | tf_op jit(solution)/shard_map/ppermute | solution.py:29
  43.7 61.9 %collective-permute-start.5 = (f32[2,1,256,256]{3,2,1,0:T(8,128)}, f32[2,1,256,256]{3,2,1,0:T(8,128)S(1)}, u32[]{:S(2)}, u32[]{:S(2)}) collective-permute-start(f32[2,1,256,256]{3,2,1,0:T(8,128)} %get-tuple-element.8), channel_id=1, source_target_pairs={{0,1},{2,3},{4,5},{6,7},{8,9},{10,11},{12,13},{14,15},{16,17},{18,... | collective-permute-start | bytes 1572872 | tf_op jit(solution)/shard_map/ppermute | solution.py:27
where the time goes:
time: 110 us
  blocking collectives  41 us (37%)
  local copies, waits for them, and re-layouts  29.3 us (27%)
  other arithmetic  19.8 us (18%)
  starting transfers between devices  18.8 us (17%)
    psum x1, blocking collectives, local(): lax.psum(patch_total(first_term + second) * factor, ('member', 'slab'))  41 us
    ppermute x3, starting transfers between devices, with_halo(): lax.ppermute(tail, axis, [(i, (i + 1) % count) for i in range(ends)])  14.9 us
    add x1, local copies, waits for them, and re-layouts, local(): first_term + second  10.8 us
    reshape x1, local copies, waits for them, and re-layouts, expand_params(): jnp.broadcast_to(table[:, None, :, None], (PX, SX, PY, SY)).reshape(NX, NY)  8.39 us
    concatenate x3, other arithmetic, with_halo(): jnp.concatenate([lax.ppermute(tail, axis, [(i, (i + 1) % count) for i in...  5.74 us
    sub x3, other arithmetic, laplace_rim(): return summed - 6.0 * center  5.14 us
    slice x2, local copies, waits for them, and re-layouts, with_halo(): lax.slice_in_dim(cells, cells.shape[dim] - width, cells.shape[dim], axis=...  4.61 us
    reduce_sum x1, other arithmetic, patch_total(): return jnp.sum(field.reshape(PX, SX, PY, SY), axis=(1, 3))  4.01 us
  transfers between devices with their start and end apart: 6, of which 0 were waited for; matrix products, arithmetic and copies ran while one was open for 31% of the time, Pallas kernels for 0%

commit v1 on v0

v1 whole, which is shorter than its diff:
```python
import functools

import jax
import jax.numpy as jnp
from jax import lax
from jax.experimental import pallas as pl
from jax.experimental.pallas import tpu as pltpu
from jax.sharding import PartitionSpec as P

MESH = pl.DeviceIdType.MESH
HIGH = lax.Precision.HIGHEST
PAD = 8
ROWS = 16
CHUNKS = 4

feed_rate = 0.035
substrate_diffusion = 0.16
activator_diffusion = 0.08


def bits_of(count):
    return [1 << i for i in range((count - 1).bit_length())]


def spread(rows, cols):
    r = lax.broadcasted_iota(jnp.int32, (rows, cols), 0)
    c = lax.broadcasted_iota(jnp.int32, (rows, cols), 1)
    if rows >= cols:
        size = rows // cols
        hit = (r >= c * size) & (r < (c + 1) * size)
    else:
        size = cols // rows
        hit = (c >= r * size) & (c < (r + 1) * size)
    return hit.astype(jnp.float32)


def dot(a, b):
    return jnp.dot(a, b, precision=HIGH, preferred_element_type=jnp.float32)


def kernel(
    n, members, ck_hbm, la_hbm, rate_ref, pert_ref, out_hbm, grad_ref,
    ck, la, mi, ob, decay, cell, gbuf, gsum,
    local_sem, in_send, in_recv, mid_send, mid_recv, g_send, g_recv, out_sem,
):
    nz, nx, ny = ob.shape[1], ob.shape[2], ob.shape[3]
    px, py = rate_ref.shape
    chunk = nx // CHUNKS
    idx = lax.axis_index("slab")
    mem = lax.axis_index("member")
    partners = [("slab", lax.bitwise_xor(idx, b)) for b in bits_of(n)]
    partners += [("member", lax.bitwise_xor(mem, b)) for b in bits_of(members)]
    has = {0: idx > 0, 1: idx < n - 1}
    peer = {0: idx - 1, 1: idx + 1}
    halo = {0: 0, 1: nz + 1}
    edge = {0: nz, 1: 1}

    loads = [
        pltpu.make_async_copy(src.at[0], dst.at[:, pl.ds(1, nz), pl.ds(PAD, nx), :], local_sem.at[i])
        for i, (src, dst) in enumerate(((ck_hbm, ck), (la_hbm, la)))
    ]
    for load in loads:
        load.start()

    barrier = pltpu.get_barrier_semaphore()
    greeted = [("slab", lax.rem(idx + j, n)) for j in range(1, n)]
    greeted += [p for p in partners if p[0] == "member"]
    for axis, who in greeted:
        pl.semaphore_signal(barrier, inc=1, device_id={axis: who}, device_id_type=MESH)
    pl.semaphore_wait(barrier, len(greeted))

    def in_copy(side, c, which):
        src, dst = ((ck_hbm, ck), (la_hbm, la))[which]
        return pltpu.make_async_remote_copy(
            src_ref=src.at[0, :, edge[side] - 1, pl.ds(c * chunk, chunk), :],
            dst_ref=dst.at[:, halo[side], pl.ds(PAD + c * chunk, chunk), :],
            send_sem=in_send.at[side, c, which],
            recv_sem=in_recv.at[side, c, which],
            device_id={"slab": peer[1 - side]},
            device_id_type=MESH,
        )

    def mid_copy(side, c):
        return pltpu.make_async_remote_copy(
            src_ref=mi.at[:, edge[side], pl.ds(PAD + c * chunk, chunk), :],
            dst_ref=mi.at[:, halo[side], pl.ds(PAD + c * chunk, chunk), :],
            send_sem=mid_send.at[side, c],
            recv_sem=mid_recv.at[side, c],
            device_id={"slab": peer[1 - side]},
            device_id_type=MESH,
        )

    def on_send(do):
        for side in (0, 1):
            @pl.when(has[1 - side])
            def _(side=side):
                do(side)

    def on_recv(do):
        for side in (0, 1):
            @pl.when(has[side])
            def _(side=side):
                do(side)

    for c in range(CHUNKS):
        for which in (0, 1):
            on_send(lambda side: in_copy(side, c, which).start())

    zero_rows = jnp.zeros((2, nz, PAD, ny), jnp.float32)
    for ref in (ck, la, mi):
        ref[:, 1 : nz + 1, 0:PAD, :] = zero_rows
        ref[:, 1 : nz + 1, PAD + nx : 2 * PAD + nx, :] = zero_rows
    for side in (0, 1):
        @pl.when(jnp.logical_not(has[side]))
        def _(side=side):
            zero = jnp.zeros((2, 2 * PAD + nx, ny), jnp.float32)
            ck[:, halo[side]] = zero
            la[:, halo[side]] = zero

    factor = 1.0 + pert_ref[0]
    decay[...] = dot(dot(spread(nx, px), rate_ref[...] * factor), spread(py, ny))
    for load in loads:
        load.wait()

    col = lax.broadcasted_iota(jnp.int32, (ROWS, ny), 1)
    first, last = col == 0, col == ny - 1

    def ring(ref, s, z, r):
        x = ref[s, z, pl.ds(r, ROWS + 2 * PAD), :]
        c = x[PAD : PAD + ROWS]
        total = x[PAD - 1 : PAD - 1 + ROWS] + x[PAD + 1 : PAD + 1 + ROWS]
        total = total + jnp.where(first, 0.0, pltpu.roll(c, 1, 1))
        total = total + jnp.where(last, 0.0, pltpu.roll(c, ny - 1, 1))
        return c, total

    def rows_of(ref, s, z, r):
        return ref[s, z, pl.ds(r + PAD, ROWS), :]

    def laplace(ref, s, z, r, low, high):
        c, total = ring(ref, s, z, r)
        if low:
            total = total + rows_of(ref, s, z - 1, r)
        if high:
            total = total + rows_of(ref, s, z + 1, r)
        return c, total - 6.0 * c

    def pull(um, vm, a, b, la_a, la_b, k):
        v2 = vm * vm
        uv2 = 2.0 * (um * vm)
        new_a = a + substrate_diffusion * la_a - (v2 + feed_rate) * a + v2 * b
        new_b = b + activator_diffusion * la_b - uv2 * a + (uv2 - feed_rate - k) * b
        return new_a, new_b

    def mid_block(r):
        k = decay[pl.ds(r, ROWS), :]
        g = None
        for z in range(1, nz + 1):
            u, lu = laplace(ck, 0, z, r, True, True)
            v, lv = laplace(ck, 1, z, r, True, True)
            react = u * v * v
            um = u + substrate_diffusion * lu - react + feed_rate * (1.0 - u)
            vm = v + activator_diffusion * lv + react - (feed_rate + k) * v
            a, l_a = laplace(la, 0, z, r, True, True)
            b, l_b = laplace(la, 1, z, r, True, True)
            new_a, new_b = pull(um, vm, a, b, l_a, l_b, k)
            mi[0, z, pl.ds(r + PAD, ROWS), :] = new_a
            mi[1, z, pl.ds(r + PAD, ROWS), :] = new_b
            term = vm * b + v * new_b
            g = term if g is None else g + term
        cell[pl.ds(r, ROWS), :] = g

    def early_block(r):
        k = decay[pl.ds(r, ROWS), :]
        for z in range(1, nz + 1):
            u, v = rows_of(ck, 0, z, r), rows_of(ck, 1, z, r)
            a, l_a = laplace(mi, 0, z, r, z > 1, z < nz)
            b, l_b = laplace(mi, 1, z, r, z > 1, z < nz)
            new_a, new_b = pull(u, v, a, b, l_a, l_b, k)
            ob[0, z - 1, pl.ds(r, ROWS), :] = new_a
            ob[1, z - 1, pl.ds(r, ROWS), :] = new_b

    def blocks(c, body):
        def step(i, carry):
            body(pl.multiple_of(c * chunk + i * ROWS, ROWS))
            return carry

        lax.fori_loop(0, chunk // ROWS, step, 0)

    for c in range(CHUNKS):
        for which in (0, 1):
            on_recv(lambda side: in_copy(side, c, which).wait_recv())
        blocks(c, mid_block)
        if c == 0:
            on_send(lambda side: mid_copy(side, 0).start())

    total = dot(dot(spread(px, nx), cell[...]), spread(ny, py))
    gsum[0] = total * factor * (-1.0 / members)

    def g_copy(i):
        axis, who = partners[i]
        return pltpu.make_async_remote_copy(
            src_ref=gsum.at[i],
            dst_ref=gbuf.at[i],
            send_sem=g_send.at[i],
            recv_sem=g_recv.at[i],
            device_id={axis: who},
            device_id_type=MESH,
        )

    if partners:
        g_copy(0).start()
    for c in range(1, CHUNKS):
        on_send(lambda side: mid_copy(side, c).start())

    steps = max(CHUNKS, len(partners))
    for i in range(steps):
        if i < CHUNKS:
            blocks(i, early_block)
        if i < len(partners):
            g_copy(i).wait_recv()
            gsum[i + 1] = gsum[i] + gbuf[i]
            if i + 1 < len(partners):
                g_copy(i + 1).start()
    grad_ref[...] = gsum[len(partners)]

    def out_copy(c):
        rows = pl.ds(c * chunk, chunk)
        return pltpu.make_async_copy(ob.at[:, :, rows, :], out_hbm.at[0, :, :, rows, :], out_sem.at[c])

    scales = (substrate_diffusion, activator_diffusion)
    for c in range(CHUNKS):
        def add(side):
            mid_copy(side, c).wait_recv()
            for s in (0, 1):
                ob[s, (0, nz - 1)[side], pl.ds(c * chunk, chunk), :] += (
                    scales[s] * mi[s, halo[side], pl.ds(PAD + c * chunk, chunk), :]
                )

        on_recv(add)
        out_copy(c).start()

    for c in range(CHUNKS):
        for which in (0, 1):
            on_send(lambda side: in_copy(side, c, which).wait_send())
        on_send(lambda side: mid_copy(side, c).wait_send())
        out_copy(c).wait()
    for i in range(len(partners)):
        g_copy(i).wait_send()


def solution(mesh):
    n, members = mesh.shape["slab"], mesh.shape["member"]
    count = len(bits_of(n)) + len(bits_of(members))

    def local(checkpoint, adjoint_late, rate_params, perturbation):
        _, _, nz, nx, ny = checkpoint.shape
        px, py = rate_params.shape
        f32 = jnp.float32
        field = pltpu.VMEM((2, nz + 2, nx + 2 * PAD, ny), f32)
        dma = pltpu.SemaphoreType.DMA
        return pl.pallas_call(
            functools.partial(kernel, n, members),
            out_shape=(
                jax.ShapeDtypeStruct(checkpoint.shape, f32),
                jax.ShapeDtypeStruct((px, py), f32),
            ),
            in_specs=[
                pl.BlockSpec(memory_space=pl.ANY),
                pl.BlockSpec(memory_space=pl.ANY),
                pl.BlockSpec(memory_space=pltpu.VMEM),
                pl.BlockSpec(memory_space=pltpu.VMEM),
            ],
            out_specs=(
                pl.BlockSpec(memory_space=pl.ANY),
                pl.BlockSpec(memory_space=pltpu.VMEM),
            ),
            scratch_shapes=[
                field,
                field,
                field,
                pltpu.VMEM((2, nz, nx, ny), f32),
                pltpu.VMEM((nx, ny), f32),
                pltpu.VMEM((nx, ny), f32),
                pltpu.VMEM((count, px, py), f32),
                pltpu.VMEM((count + 1, px, py), f32),
                dma((2,)),
                dma((2, CHUNKS, 2)),
                dma((2, CHUNKS, 2)),
                dma((2, CHUNKS)),
                dma((2, CHUNKS)),
                dma((count,)),
                dma((count,)),
                dma((CHUNKS,)),
            ],
            compiler_params=pltpu.CompilerParams(collective_id=0, has_side_effects=True),
        )(checkpoint, adjoint_late, rate_params, perturbation)

    return jax.shard_map(
        local,
        mesh=mesh,
        in_specs=(
            P("member", None, "slab", None, None),
            P("member", None, "slab", None, None),
            P(),
            P("member", None, None),
        ),
        out_specs=(P("member", None, "slab", None, None), P()),
        check_vma=False,
    )
```

time: 110 us -> 52.1 us (0.47)
  Pallas kernels: 0 us -> 48.3 us
  blocking collectives: 41 us -> 0 us
  local copies, waits for them, and re-layouts: 29.3 us -> 2.91 us
  other arithmetic: 19.8 us -> 0 us
  starting transfers between devices: 18.8 us -> 0 us
    pallas_call x0 -> x1, Pallas kernels: none -> 48.3 us  [local(): pl.pallas_call(functools.partial(kernel, n, members), out_shape=(jax.Shap...]
    psum x1 -> x0, blocking collectives: 41 us -> none  [local(): lax.psum(patch_total(first_term + second) * factor, ('member', 'slab'))]
    ppermute x6 -> x0, starting transfers between devices: 18.8 us -> none  [the longest x3 14.9 us: with_halo(): lax.ppermute(tail, axis, [(i, (i + 1) % count) for i in range(ends)])]
    add x1 -> x0, local copies, waits for them, and re-layouts: 10.8 us -> none  [local(): first_term + second]
    reshape x1 -> x0, local copies, waits for them, and re-layouts: 8.39 us -> none  [expand_params(): jnp.broadcast_to(table[:, None, :, None], (PX, SX, PY, SY)).reshape(NX, NY)]
    concatenate x3 -> x0, other arithmetic: 5.74 us -> none  [with_halo(): jnp.concatenate([lax.ppermute(tail, axis, [(i, (i + 1) % count) for i in...]
    sub x3 -> x0, other arithmetic: 5.14 us -> none  [laplace_rim(): return summed - 6.0 * center]
    slice x2 -> x0, local copies, waits for them, and re-layouts: 4.61 us -> none  [with_halo(): lax.slice_in_dim(cells, cells.shape[dim] - width, cells.shape[dim], axis=...]
  transfers between devices with their start and end apart: 6 -> 0, of which waited for: 0 -> 0; matrix products, arithmetic and copies ran while one was open for 31% -> 0% of each run, Pallas kernels for 0% -> 0%
where the time goes in v1:
time: 52.1 us; the launch traced here: 51.8 us
  Pallas kernels  48.3 us (93%)
  local copies, waits for them, and re-layouts  2.91 us (6%)
  between operations  0.65 us (1%)
    pallas_call x1, Pallas kernels, local(): pl.pallas_call(functools.partial(kernel, n, members), out_shape=(jax.Shap...  48.3 us
    unnamed x4, local copies, waits for them, and re-layouts  2.91 us

profile of v1, /device:TPU:0, one launch (start us, length us, event | category | flops | bytes accessed | tf_op | source)
XLA Modules:
  0.0 51.8 jit_solution(8826182180992408769)
XLA Ops:
  0.6 48.3 %shard_map.59 = (f32[1,2,2,256,256]{4,3,2,1,0:T(8,128)}, f32[64,64]{1,0:T(8,128)}) custom-call(f32[1,2,2,256,256]{4,3,2,1,0:T(8,128)} %ck_hbm.1, f32[1,2,2,256,256]{4,3,2,1,0:T(8,128)} %la_hbm.1, f32[64,64]{1,0:T(8,128)} %rate_ref.1, f32[1,64,64]{2,1,0:T(8,128)} %pert_ref.1), custom_call_target="tpu_custom_call" | custom-call | tf_op jit(solution)/shard_map/pallas_call | solution.py:261
  48.9 0.0 copy-start
  48.9 2.3 %copy.8 = f32[1,2,2,256,256]{4,3,2,1,0:T(8,128)} copy(f32[1,2,2,256,256]{4,3,2,1,0:T(8,128)} %get-tuple-element.4) | data formatting | bytes 2097152
  51.2 0.0 copy-done
  51.2 0.6 %copy.9 = f32[64,64]{1,0:T(8,128)} copy(f32[64,64]{1,0:T(8,128)S(1)} %copy-done) | data formatting | bytes 32768
Async XLA Ops:
  48.9 2.3 %copy-start = (f32[64,64]{1,0:T(8,128)S(1)}, f32[64,64]{1,0:T(8,128)}, u32[]{:S(2)}) copy-start(f32[64,64]{1,0:T(8,128)} %get-tuple-element.5) | copy-start | bytes 49156

commit v2 on v1

--- a/solution.py
+++ b/solution.py
@@ -11,15 +11,22 @@
 HIGH = lax.Precision.HIGHEST
 PAD = 8
 ROWS = 16
-CHUNKS = 4
+CHUNKS = 8
 
 feed_rate = 0.035
 substrate_diffusion = 0.16
 activator_diffusion = 0.08
 
 
-def bits_of(count):
-    return [1 << i for i in range((count - 1).bit_length())]
+def stages_of(n, members):
+    stages, slot = [], 0
+    for axis, count in (("member", members), ("slab", n)):
+        bit = 1
+        while bit < count:
+            radix = 4 if bit * 4 <= count else 2
+            stages.append((axis, [bit * j for j in range(1, radix)], slot))
+            bit, slot = bit * radix, slot + radix - 1
+    return stages, slot
 
 
 def spread(rows, cols):
@@ -40,7 +47,7 @@
 
 def kernel(
     n, members, ck_hbm, la_hbm, rate_ref, pert_ref, out_hbm, grad_ref,
-    ck, la, mi, ob, decay, cell, gbuf, gsum,
+    ck, la, mi, ob, decay, weight, cell, gbuf, gsum,
     local_sem, in_send, in_recv, mid_send, mid_recv, g_send, g_recv, out_sem,
 ):
     nz, nx, ny = ob.shape[1], ob.shape[2], ob.shape[3]
@@ -48,8 +55,7 @@
     chunk = nx // CHUNKS
     idx = lax.axis_index("slab")
     mem = lax.axis_index("member")
-    partners = [("slab", lax.bitwise_xor(idx, b)) for b in bits_of(n)]
-    partners += [("member", lax.bitwise_xor(mem, b)) for b in bits_of(members)]
+    stages, _ = stages_of(n, members)
     has = {0: idx > 0, 1: idx < n - 1}
     peer = {0: idx - 1, 1: idx + 1}
     halo = {0: 0, 1: nz + 1}
@@ -64,7 +70,9 @@
 
     barrier = pltpu.get_barrier_semaphore()
     greeted = [("slab", lax.rem(idx + j, n)) for j in range(1, n)]
-    greeted += [p for p in partners if p[0] == "member"]
+    for axis, offsets, _ in stages:
+        if axis == "member":
+            greeted += [(axis, lax.bitwise_xor(mem, j)) for j in offsets]
     for axis, who in greeted:
         pl.semaphore_signal(barrier, inc=1, device_id={axis: who}, device_id_type=MESH)
     pl.semaphore_wait(barrier, len(greeted))
@@ -118,6 +126,7 @@
             la[:, halo[side]] = zero
 
     factor = 1.0 + pert_ref[0]
+    weight[...] = dot(dot(spread(nx, px), factor * (-1.0 / members)), spread(py, ny))
     decay[...] = dot(dot(spread(nx, px), rate_ref[...] * factor), spread(py, ny))
     for load in loads:
         load.wait()
@@ -167,7 +176,7 @@
             mi[1, z, pl.ds(r + PAD, ROWS), :] = new_b
             term = vm * b + v * new_b
             g = term if g is None else g + term
-        cell[pl.ds(r, ROWS), :] = g
+        cell[pl.ds(r, ROWS), :] = g * weight[pl.ds(r, ROWS), :]
 
     def early_block(r):
         k = decay[pl.ds(r, ROWS), :]
@@ -186,43 +195,65 @@
 
         lax.fori_loop(0, chunk // ROWS, step, 0)
 
+    patch_rows = px // CHUNKS
+    half = patch_rows // 2
+
+    def packed_sums(c):
+        sums = dot(spread(patch_rows, chunk), cell[pl.ds(c * chunk, chunk), :])
+        size = ny // py
+        r = lax.broadcasted_iota(jnp.int32, (ny, 2 * py), 0)
+        q = lax.broadcasted_iota(jnp.int32, (ny, 2 * py), 1) * size
+        upper = ((r >= q) & (r < q + size)).astype(jnp.float32)
+        lower = ((r + ny >= q) & (r + ny < q + size)).astype(jnp.float32)
+        return dot(sums[:half], upper) + dot(sums[half:], lower)
+
+    def g_copies(s):
+        axis, offsets, slot = stages[s]
+        own = mem if axis == "member" else idx
+        return [
+            pltpu.make_async_remote_copy(
+                src_ref=gsum.at[s],
+                dst_ref=gbuf.at[slot + j],
+                send_sem=g_send.at[slot + j],
+                recv_sem=g_recv.at[slot + j],
+                device_id={axis: lax.bitwise_xor(own, offset)},
+                device_id_type=MESH,
+            )
+            for j, offset in enumerate(offsets)
+        ]
+
+    def add_up(s):
+        _, offsets, slot = stages[s]
+        for copy in g_copies(s):
+            copy.wait_recv()
+        value = gsum[s] + gbuf[slot]
+        if len(offsets) == 3:
+            value = value + (gbuf[slot + 1] + gbuf[slot + 2])
+        gsum[s + 1] = value
+
     for c in range(CHUNKS):
         for which in (0, 1):
             on_recv(lambda side: in_copy(side, c, which).wait_recv())
         blocks(c, mid_block)
+        gsum[0, pl.ds(c * half, half), :] = packed_sums(c)
         if c == 0:
             on_send(lambda side: mid_copy(side, 0).start())
 
-    total = dot(dot(spread(px, nx), cell[...]), spread(ny, py))
-    gsum[0] = total * factor * (-1.0 / members)
-
-    def g_copy(i):
-        axis, who = partners[i]
-        return pltpu.make_async_remote_copy(
-            src_ref=gsum.at[i],
-            dst_ref=gbuf.at[i],
-            send_sem=g_send.at[i],
-            recv_sem=g_recv.at[i],
-            device_id={axis: who},
-            device_id_type=MESH,
-        )
-
-    if partners:
-        g_copy(0).start()
-    for c in range(1, CHUNKS):
-        on_send(lambda side: mid_copy(side, c).start())
-
-    steps = max(CHUNKS, len(partners))
-    for i in range(steps):
-        if i < CHUNKS:
-            blocks(i, early_block)
-        if i < len(partners):
-            g_copy(i).wait_recv()
-            gsum[i + 1] = gsum[i] + gbuf[i]
-            if i + 1 < len(partners):
-                g_copy(i + 1).start()
-    grad_ref[...] = gsum[len(partners)]
-
+    sent, early = 1, 0
+    for s in range(max(len(stages), 1)):
+        if s > 0:
+            add_up(s - 1)
+        if s < len(stages):
+            for copy in g_copies(s):
+                copy.start()
+        upto = CHUNKS if s >= len(stages) - 1 else 1 + (CHUNKS - 1) * (s + 1) // max(len(stages), 1)
+        for c in range(sent, upto):
+            on_send(lambda side: mid_copy(side, c).start())
+        sent = max(sent, upto)
+        upto = CHUNKS if s >= len(stages) - 1 else CHUNKS * (s + 1) // len(stages)
+        for c in range(early, upto):
+            blocks(c, early_block)
+        early = max(early, upto)
     def out_copy(c):
         rows = pl.ds(c * chunk, chunk)
         return pltpu.make_async_copy(ob.at[:, :, rows, :], out_hbm.at[0, :, :, rows, :], out_sem.at[c])
@@ -239,18 +270,26 @@
         on_recv(add)
         out_copy(c).start()
 
+    if stages:
+        add_up(len(stages) - 1)
+    for c in range(CHUNKS):
+        value = gsum[len(stages), pl.ds(c * half, half), :]
+        grad_ref[pl.ds(c * patch_rows, half), :] = value[:, :py]
+        grad_ref[pl.ds(c * patch_rows + half, half), :] = pltpu.roll(value, py, 1)[:, :py]
+
     for c in range(CHUNKS):
         for which in (0, 1):
             on_send(lambda side: in_copy(side, c, which).wait_send())
         on_send(lambda side: mid_copy(side, c).wait_send())
         out_copy(c).wait()
-    for i in range(len(partners)):
-        g_copy(i).wait_send()
+    for s in range(len(stages)):
+        for copy in g_copies(s):
+            copy.wait_send()
 
 
 def solution(mesh):
     n, members = mesh.shape["slab"], mesh.shape["member"]
-    count = len(bits_of(n)) + len(bits_of(members))
+    stages, slots = stages_of(n, members)
 
     def local(checkpoint, adjoint_late, rate_params, perturbation):
         _, _, nz, nx, ny = checkpoint.shape
@@ -281,15 +320,16 @@
                 pltpu.VMEM((2, nz, nx, ny), f32),
                 pltpu.VMEM((nx, ny), f32),
                 pltpu.VMEM((nx, ny), f32),
-                pltpu.VMEM((count, px, py), f32),
-                pltpu.VMEM((count + 1, px, py), f32),
+                pltpu.VMEM((nx, ny), f32),
+                pltpu.VMEM((slots, px // 2, 2 * py), f32),
+                pltpu.VMEM((len(stages) + 1, px // 2, 2 * py), f32),
                 dma((2,)),
                 dma((2, CHUNKS, 2)),
                 dma((2, CHUNKS, 2)),
                 dma((2, CHUNKS)),
                 dma((2, CHUNKS)),
-                dma((count,)),
-                dma((count,)),
+                dma((slots,)),
+                dma((slots,)),
                 dma((CHUNKS,)),
             ],
             compiler_params=pltpu.CompilerParams(collective_id=0, has_side_effects=True),

time: 52.1 us -> 50.3 us (0.965)
  Pallas kernels: 48.3 us -> 46.5 us
    pallas_call x1, Pallas kernels: 48.3 us -> 46.5 us  [local(): pl.pallas_call(functools.partial(kernel, n, members), out_shape=(jax.Shap...]
where the time goes in v2:
time: 50.3 us; the launch traced here: 50.1 us
  Pallas kernels  46.5 us (92%)
  local copies, waits for them, and re-layouts  2.91 us (6%)
  between operations  0.65 us (1%)
    pallas_call x1, Pallas kernels, local(): pl.pallas_call(functools.partial(kernel, n, members), out_shape=(jax.Shap...  46.5 us
    unnamed x4, local copies, waits for them, and re-layouts  2.91 us

profile of v2, /device:TPU:0, one launch (start us, length us, event | category | flops | bytes accessed | tf_op | source)
XLA Modules:
  0.0 50.1 jit_solution(14689731731416998584)
XLA Ops:
  0.6 46.5 %shard_map.59 = (f32[1,2,2,256,256]{4,3,2,1,0:T(8,128)}, f32[64,64]{1,0:T(8,128)}) custom-call(f32[1,2,2,256,256]{4,3,2,1,0:T(8,128)} %ck_hbm.1, f32[1,2,2,256,256]{4,3,2,1,0:T(8,128)} %la_hbm.1, f32[64,64]{1,0:T(8,128)} %rate_ref.1, f32[1,64,64]{2,1,0:T(8,128)} %pert_ref.1), custom_call_target="tpu_custom_call" | custom-call | tf_op jit(solution)/shard_map/pallas_call | solution.py:300
  47.2 0.0 copy-start
  47.2 2.3 %copy.8 = f32[1,2,2,256,256]{4,3,2,1,0:T(8,128)} copy(f32[1,2,2,256,256]{4,3,2,1,0:T(8,128)} %get-tuple-element.4) | data formatting | bytes 2097152
  49.5 0.0 copy-done
  49.5 0.6 %copy.9 = f32[64,64]{1,0:T(8,128)} copy(f32[64,64]{1,0:T(8,128)S(1)} %copy-done) | data formatting | bytes 32768
Async XLA Ops:
  47.2 2.3 %copy-start = (f32[64,64]{1,0:T(8,128)S(1)}, f32[64,64]{1,0:T(8,128)}, u32[]{:S(2)}) copy-start(f32[64,64]{1,0:T(8,128)} %get-tuple-element.5) | copy-start | bytes 49156
